TPU v7x, 32 devices: a whole 2x2x4 slice. The times are simulated.
32 devices in a mesh: gz: 4 (over y, x), gy: 8 (over z, core).
Axes of the slice: x: 2, y: 2, z: 4, core: 2. Of those that a mesh axis runs over, the one named last changes fastest.
Arguments:
- velocity: float32 [3, 32, 128, 768], P(None, 'gz', 'gy'), may hold values from -6 to 6
- forces: bfloat16 [1024, 3, 128], P(('gz', 'gy')), may hold values from -6 to 6
- kernels: bfloat16 [1024, 128, 256], P(('gz', 'gy')), may hold values from -0.5 to 0.5
- owners: int32 [1024, 1], P(('gz', 'gy')), may hold values from 0 to 7; in each aligned block of 32 rows (0 to 31, 32 to 63, ...) at most 8 rows name the same one
- blocks: int32 [1024], P(('gz', 'gy')), may hold values from 0 to 383
- counts: int32 [32], P(('gz', 'gy')), may hold values from 16 to 32, as said below
Outputs:
- velocity_next: float32 [3, 32, 128, 768], P(None, 'gz', 'gy')
- patch_velocity: float32 [1024, 3, 128], P(('gz', 'gy'))
Inputs may be any that keep to these rules, and one draw needn't show every extreme that they name: `owners`: owners are gy indices in the holder's own row along gz; among the 32 patches of one device at most 8 share an owner, and some owner has exactly 8. `blocks`: A cell block index within the owner's part of the grid. `counts`: live patches come first in a device's slots; some device has all 32 live.
All inputs are finite; a program needn't handle non-finite values.
Results may differ from a plain program's by a relative error of at most 0.0027.
Values may be sent and summed in bfloat16 or wider, within the bound.
A program may use at most 64 MiB of HBM per device.

v0:
```python
import functools

import jax
import jax.numpy as jnp
from jax import lax
from jax.experimental import pallas as pl
from jax.experimental.pallas import tpu as pltpu
from jax.sharding import PartitionSpec as P

time_step = 0.25
vmem_bytes = 67043328
viscosity = 0.5
MESH = pl.DeviceIdType.MESH
f32 = jnp.float32
bf16 = jnp.bfloat16


def iota(shape, dim):
    return lax.broadcasted_iota(jnp.int32, shape, dim)


def step_kernel(width, depth, room, vel_hbm, force_hbm, kern_hbm, own_hbm, blk_hbm, cnt_hbm,
                fresh, kv, held_ref,
                v, force_ref, own_ref, blk_ref, cnt_ref, cells16, id_out, id_in, send, recv, back, mine,
                zs, zr, ys, yr,
                in_sem, kern_sem, id_send, id_recv, go_send, go_recv, re_send, re_recv, h_send, h_recv):
    me = lax.axis_index("gy")
    gz = lax.axis_index("gz")
    comps, planes, rows, xcells = v.shape
    _, slots, pts = force_ref.shape
    cells = kv.shape[1]
    nx = xcells // cells
    zy = planes * rows
    total = width * room
    body = comps * cells
    coef = time_step * viscosity
    half = time_step * 0.5
    group = 8
    groups = slots // group
    span = group * pts

    gets = [pltpu.make_async_copy(src, dst, in_sem.at[i]) for i, (src, dst) in enumerate((
        (own_hbm, own_ref), (blk_hbm, blk_ref), (cnt_hbm, cnt_ref), (force_hbm, force_ref), (vel_hbm, v)))]
    get_kern = [pltpu.make_async_copy(kern_hbm.at[pl.ds(g * span, span)], kv.at[pl.ds(g * span, span)],
                                      kern_sem.at[g]) for g in range(groups)]
    for copy in gets + get_kern:
        copy.start()

    barrier = pltpu.get_barrier_semaphore()
    for k in range(1, width):
        pl.semaphore_signal(barrier, inc=1, device_id={"gy": lax.rem(me + k, width)}, device_id_type=MESH)
    z_lo, z_hi = gz > 0, gz < depth - 1
    y_lo, y_hi = me > 0, me < width - 1

    @pl.when(z_lo)
    def _():
        pl.semaphore_signal(barrier, inc=1, device_id={"gz": gz - 1}, device_id_type=MESH)

    @pl.when(z_hi)
    def _():
        pl.semaphore_signal(barrier, inc=1, device_id={"gz": gz + 1}, device_id_type=MESH)

    for copy in gets[:3]:
        copy.wait()
    rowi, coli = iota((slots, slots), 0), iota((slots, slots), 1)
    own_r = jnp.broadcast_to(own_ref[...].astype(f32), (slots, slots))
    own_c = jnp.sum(jnp.where(rowi == coli, own_r, 0.0), axis=1, keepdims=True)
    same = jnp.where(own_r == own_c, 1.0, 0.0)
    rank_c = jnp.sum(jnp.where(coli < rowi, same, 0.0), axis=1, keepdims=True)
    rank_r = jnp.sum(jnp.where(rowi < coli, same, 0.0), axis=0, keepdims=True)
    count = cnt_ref[...]
    me_f = me.astype(f32)

    def slot_of(owner, rank, index):
        offset = owner - me_f
        offset = jnp.where(offset < 0.0, offset + width, offset)
        return jnp.where(index < count, offset * room + rank, -1.0)

    slot_c = slot_of(own_c, rank_c, iota((slots, 1), 0))
    slot_r = slot_of(own_r[0:1, :], rank_r, iota((1, slots), 1))
    chosen = iota((total, slots), 0).astype(f32) == slot_r
    ids = jnp.sum(jnp.where(chosen, blk_ref[...].astype(f32), 0.0), axis=1, keepdims=True)
    id_hi = jnp.floor(ids * (1.0 / 128.0))
    id_lo = ids - 128.0 * id_hi
    tail = jnp.where(iota((total, 128), 1) < 64, id_lo, id_hi)
    id_out[...] = tail.reshape(width, room, 128).astype(bf16)

    gets[4].wait()
    for c in range(comps):
        zs[0, c] = v[c, 0].astype(bf16)
        zs[1, c] = v[c, planes - 1].astype(bf16)
        for side, y in ((0, 0), (1, rows - 1)):
            ys[side, c] = jnp.concatenate([v[c, z, y:y + 1, :] for z in range(planes)], axis=0).astype(bf16)

    pl.semaphore_wait(barrier, width - 1 + z_lo.astype(jnp.int32) + z_hi.astype(jnp.int32))

    order = sorted(range(1, width), key=lambda k: -min(k, width - k))

    def out(src, dst, send_sem, recv_sem, back_by=False):
        copies = {}
        for k in order:
            shift = width - k if back_by else k
            copies[k] = pltpu.make_async_remote_copy(
                src_ref=src.at[k], dst_ref=dst.at[k], send_sem=send_sem.at[k], recv_sem=recv_sem.at[k],
                device_id={"gy": lax.rem(me + shift, width)}, device_id_type=MESH)
            copies[k].start()
        return copies

    tell = out(id_out, id_in, id_send, id_recv)
    id_in[0] = id_out[0]

    def halo(src, dst, sem, axis, target):
        return pltpu.make_async_remote_copy(
            src_ref=src, dst_ref=dst, send_sem=h_send.at[sem], recv_sem=h_recv.at[sem],
            device_id={axis: target}, device_id_type=MESH)

    z_down = halo(zs.at[0], zr.at[1], 1, "gz", gz - 1)
    z_up = halo(zs.at[1], zr.at[0], 0, "gz", gz + 1)
    y_down = halo(ys.at[0], yr.at[1], 3, "gy", me - 1)
    y_up = halo(ys.at[1], yr.at[0], 2, "gy", me + 1)
    for there, copy in ((z_lo, z_down), (z_hi, z_up), (y_lo, y_down), (y_hi, y_up)):
        pl.when(there)(copy.start)

    gets[3].wait()
    line8 = iota((group, pts), 0)
    parts = []
    for g in range(groups):
        left = jnp.concatenate([jnp.concatenate([
            jnp.where(line8 == i, force_ref[c, g * group + i:g * group + i + 1, :].astype(f32), 0.0)
            for i in range(group)], axis=1) for c in range(comps)], axis=0).astype(bf16)
        get_kern[g].wait()
        parts.append(jnp.dot(left, kv[g * span:(g + 1) * span, :], preferred_element_type=f32))
    spread = jnp.concatenate([
        jnp.concatenate([part[c * group:(c + 1) * group] for part in parts], axis=0)
        for c in range(comps)], axis=1).astype(bf16)
    placed = jnp.dot(jnp.where(chosen, 1.0, 0.0).astype(bf16), spread, preferred_element_type=f32)
    send[...] = placed.reshape(width, room, body).astype(bf16)

    go = out(send, recv, go_send, go_recv)
    recv[0] = send[0]

    lane = iota((rows, xcells), 1)
    line = iota((rows, xcells), 0)
    first_x, last_x = lane == 0, lane == xcells - 1
    first_y, last_y = line == 0, line == rows - 1

    def plane(z, carry):
        vx, vy, vz = v[0, z], v[1, z], v[2, z]
        xu_w = jnp.where(last_x, 0.0, coef - half * vx)
        xd_w = jnp.where(first_x, 0.0, coef + half * vx)
        yu_w = jnp.where(last_y, 0.0, coef - half * vy)
        yd_w = jnp.where(first_y, 0.0, coef + half * vy)
        zu_w = jnp.where(z == planes - 1, 0.0, coef - half * vz)
        zd_w = jnp.where(z == 0, 0.0, coef + half * vz)
        above, below = jnp.minimum(z + 1, planes - 1), jnp.maximum(z - 1, 0)
        for c in range(comps):
            mid = v[c, z]
            value = (1.0 - 6.0 * coef) * mid
            value += xu_w * pltpu.roll(mid, xcells - 1, 1) + xd_w * pltpu.roll(mid, 1, 1)
            value += yu_w * pltpu.roll(mid, rows - 1, 0) + yd_w * pltpu.roll(mid, 1, 0)
            value += zu_w * v[c, above] + zd_w * v[c, below]
            fresh[c, z] = value
        return carry

    lax.fori_loop(0, planes, plane, 0)

    for there, copy, buf, z, sign in ((z_lo, z_up, 0, 0, half), (z_hi, z_down, 1, planes - 1, -half)):
        @pl.when(there)
        def _(copy=copy, buf=buf, z=z, sign=sign):
            copy.wait_recv()
            w = coef + sign * v[2, z]
            for c in range(comps):
                fresh[c, z] += w * zr[buf, c].astype(f32)

    for there, copy, buf, y, sign in ((y_lo, y_up, 0, 0, half), (y_hi, y_down, 1, rows - 1, -half)):
        @pl.when(there)
        def _(copy=copy, buf=buf, y=y, sign=sign):
            copy.wait_recv()
            for c in range(comps):
                got = yr[buf, c].astype(f32)
                for z in range(planes):
                    w = coef + sign * v[1, z, y:y + 1, :]
                    fresh[c, z, y:y + 1, :] += w * got[z:z + 1, :]

    for k in order[::-1]:
        tell[k].wait()
    gid = id_in[...].astype(f32).reshape(total, 128)
    gid = 128.0 * gid[:, 64:65] + gid[:, 0:1]
    ids_r = jnp.sum(jnp.where(iota((total, total), 0) == iota((total, total), 1), gid, 0.0), axis=0, keepdims=True)
    place_r = (iota((zy, total), 0) * nx).astype(f32)
    place_c = (iota((total, zy), 1) * nx).astype(f32)
    puts = [jnp.where(place_r + float(b) == ids_r, time_step, 0.0).astype(bf16) for b in range(nx)]
    takes = [jnp.where(place_c + float(b) == gid, 1.0, 0.0).astype(bf16) for b in range(nx)]
    for k in order[::-1]:
        go[k].wait()
    got = recv[...].astype(f32).reshape(total, body).astype(bf16)
    for b in range(nx):
        part = jnp.dot(puts[b], got, preferred_element_type=f32)
        for c in range(comps):
            where = (c, slice(None), slice(None), slice(b * cells, (b + 1) * cells))
            value = fresh[where] + part[:, c * cells:(c + 1) * cells].reshape(planes, rows, cells)
            fresh[where] = value
            cells16[c, :, b * cells:(b + 1) * cells] = value.reshape(zy, cells).astype(bf16)
    for c in range(comps):
        part = jnp.zeros((total, cells), f32)
        for b in range(nx):
            part += jnp.dot(takes[b], cells16[c, :, b * cells:(b + 1) * cells], preferred_element_type=f32)
        back[:, :, c * cells:(c + 1) * cells] = part.reshape(width, room, cells).astype(bf16)

    home = out(back, mine, re_send, re_recv, True)
    mine[0] = back[0]

    for there, copy in ((z_lo, z_down), (z_hi, z_up), (y_lo, y_down), (y_hi, y_up)):
        pl.when(there)(copy.wait_send)
    pick = jnp.where(iota((slots, total), 1).astype(f32) == slot_c, 1.0, 0.0).astype(bf16)
    for k in order[::-1]:
        home[k].wait()
    held = mine[...].astype(f32).reshape(total, body).astype(bf16)
    held_ref[...] = jnp.dot(pick, held, preferred_element_type=f32).astype(bf16)


def sample_kernel(fresh, kv, held_ref, fresh_hbm, out_ref, out_sem):
    comps, slots, pts = out_ref.shape
    cells = kv.shape[1]
    group = 8
    put_v = pltpu.make_async_copy(fresh, fresh_hbm, out_sem)
    put_v.start()
    line8 = iota((group, pts), 0)
    for g in range(slots // group):
        part = held_ref[g * group:(g + 1) * group, :].astype(f32)
        left = jnp.concatenate([part[:, c * cells:(c + 1) * cells] for c in range(comps)], axis=0).astype(bf16)
        result = lax.dot_general(left, kv[g * group * pts:(g + 1) * group * pts, :],
                                 (((1,), (1,)), ((), ())), preferred_element_type=f32)
        for c in range(comps):
            value = jnp.zeros((group, pts), f32)
            for i in range(group):
                value = jnp.where(line8 == i, result[c * group:(c + 1) * group, i * pts:(i + 1) * pts], value)
            out_ref[c, g * group:(g + 1) * group, :] = value
    put_v.wait()


def local(velocity, forces, kernels, owners, blocks, counts):
    width, depth = lax.axis_size("gy"), lax.axis_size("gz")
    slots, comps, pts = forces.shape
    cells = kernels.shape[2]
    _, planes, rows, xcells = velocity.shape
    room = max(2, (2 * slots + width - 1) // width)
    room = (room + 7) // 8 * 8
    total, body = width * room, comps * cells
    vmem = pl.BlockSpec(memory_space=pltpu.VMEM)
    anyw = pl.BlockSpec(memory_space=pltpu.HBM)
    dma = pltpu.SemaphoreType.DMA
    each = dma((width,))
    kept = 4 * velocity.size + 2 * kernels.size + 2 * slots * body
    fresh, kv, held = pl.pallas_call(
        functools.partial(step_kernel, width, depth, room),
        out_shape=(
            pltpu.VMEM(velocity.shape, f32),
            pltpu.VMEM((slots * pts, cells), bf16),
            pltpu.VMEM((slots, body), bf16),
        ),
        in_specs=[anyw] * 6,
        out_specs=(vmem, vmem, vmem),
        scratch_shapes=[
            pltpu.VMEM(velocity.shape, f32),
            pltpu.VMEM((comps, slots, pts), bf16),
            pltpu.VMEM((1, slots), jnp.int32),
            pltpu.VMEM((1, slots), jnp.int32),
            pltpu.VMEM((1, 1), jnp.int32),
            pltpu.VMEM((comps, planes * rows, xcells), bf16),
            pltpu.VMEM((width, room, 128), bf16),
            pltpu.VMEM((width, room, 128), bf16),
            pltpu.VMEM((width, room, body), bf16),
            pltpu.VMEM((width, room, body), bf16),
            pltpu.VMEM((width, room, body), bf16),
            pltpu.VMEM((width, room, body), bf16),
            pltpu.VMEM((2, comps, rows, xcells), bf16),
            pltpu.VMEM((2, comps, rows, xcells), bf16),
            pltpu.VMEM((2, comps, planes, xcells), bf16),
            pltpu.VMEM((2, comps, planes, xcells), bf16),
            dma((5,)), dma((slots // 8,)), each, each, each, each, each, each, dma((4,)), dma((4,)),
        ],
        compiler_params=pltpu.CompilerParams(
            collective_id=0, has_side_effects=True, vmem_limit_bytes=vmem_bytes - kept - 512 * 1024),
        name="boundary_step",
    )(velocity, forces.transpose(1, 0, 2), kernels.reshape(slots * pts, cells),
      owners.reshape(1, slots), blocks.reshape(1, slots), counts.reshape(1, 1))
    fresh, sampled = pl.pallas_call(
        sample_kernel,
        out_shape=(
            jax.ShapeDtypeStruct(velocity.shape, f32),
            jax.ShapeDtypeStruct((comps, slots, pts), f32),
        ),
        in_specs=[vmem, vmem, vmem],
        out_specs=(anyw, vmem),
        scratch_shapes=[dma],
        compiler_params=pltpu.CompilerParams(vmem_limit_bytes=24 * 2**20),
        name="sample_points",
    )(fresh, kv, held)
    return fresh, sampled.transpose(1, 0, 2)


def solution(mesh):
    return jax.shard_map(
        local,
        mesh=mesh,
        in_specs=(
            P(None, "gz", "gy", None),
            P(("gz", "gy"), None, None),
            P(("gz", "gy"), None, None),
            P(("gz", "gy"), None),
            P(("gz", "gy")),
            P(("gz", "gy")),
        ),
        out_specs=(P(None, "gz", "gy", None), P(("gz", "gy"), None, None)),
        check_vma=False,
    )
```

profile of v0, /device:TPU:0, one launch (start us, length us, event | category | flops | bytes accessed | tf_op | source)
XLA Modules:
  0.0 19.3 jit_solution(1192104995148509090)
XLA Ops:
  1.3 16.2 %boundary_step.1 = (f32[3,8,16,768]{3,2,1,0:T(8,128)S(1)}, bf16[4096,256]{1,0:T(8,128)(2,1)S(1)}, bf16[32,768]{1,0:T(8,128)(2,1)S(1)}) custom-call(f32[3,8,16,768]{3,2,1,0:T(8,128)} %vel_hbm.1, bf16[3,32,128]{2,1,0:T(8,128)(2,1)} %bitcast.8, bf16[4096,256]{1,0:T(8,128)(2,1)} %bitcast.7, s32[1,32]{1,0:T(1,128)} %bitcast.9, s32[1,32]{1,0:T(1,128)} %bitcast.10, ...), custom_call_target="tpu_custom_call" | custom-call | tf_op jit(solution)/shard_map/boundary_step/pallas_call | solution.py:255
  17.5 1.8 %sample_points.1 = (f32[3,8,16,768]{3,2,1,0:T(8,128)}, f32[3,32,128]{2,1,0:T(8,128)}) custom-call(f32[3,8,16,768]{3,2,1,0:T(8,128)S(1)} %get-tuple-element.7.fresh, bf16[4096,256]{1,0:T(8,128)(2,1)S(1)} %get-tuple-element.8.kv, bf16[32,768]{1,0:T(8,128)(2,1)S(1)} %get-tuple-element.9.held_ref), custom_call_target="tpu_custom_call" | custom-call | tf_op jit(solution)/shard_map/sample_points/pallas_call | solution.py:288
where the time goes:
time: 19.4 us; the launch traced here: 19.3 us
  Pallas kernels  18 us (93%)
  between operations  1.29 us (7%)
    pallas_call x1, Pallas kernels, local(): pl.pallas_call(functools.partial(step_kernel, width, depth, room), out_sh...  16.2 us
    pallas_call x1, Pallas kernels, local(): pl.pallas_call(sample_kernel, out_shape=(jax.ShapeDtypeStruct(velocity.sh...  1.79 us

commit v1 on v0

--- a/solution.py
+++ b/solution.py
@@ -21,7 +21,7 @@
 
 def step_kernel(width, depth, room, vel_hbm, force_hbm, kern_hbm, own_hbm, blk_hbm, cnt_hbm,
                 fresh, kv, held_ref,
-                v, force_ref, own_ref, blk_ref, cnt_ref, cells16, id_out, id_in, send, recv, back, mine,
+                v, force_ref, own_ref, blk_ref, cnt_ref, cells16, left_ref, id_out, id_in, send, recv, back, mine,
                 zs, zr, ys, yr,
                 in_sem, kern_sem, id_send, id_recv, go_send, go_recv, re_send, re_recv, h_send, h_recv):
     me = lax.axis_index("gy")
@@ -39,26 +39,26 @@
     groups = slots // group
     span = group * pts
 
+    barrier = pltpu.get_barrier_semaphore()
+    for k in range(1, width):
+        pl.semaphore_signal(barrier, inc=1, device_id={"gy": lax.rem(me + k, width)}, device_id_type=MESH)
+    z_lo, z_hi = gz > 0, gz < depth - 1
+    y_lo, y_hi = me > 0, me < width - 1
+
+    @pl.when(z_lo)
+    def _():
+        pl.semaphore_signal(barrier, inc=1, device_id={"gz": gz - 1}, device_id_type=MESH)
+
+    @pl.when(z_hi)
+    def _():
+        pl.semaphore_signal(barrier, inc=1, device_id={"gz": gz + 1}, device_id_type=MESH)
+
     gets = [pltpu.make_async_copy(src, dst, in_sem.at[i]) for i, (src, dst) in enumerate((
         (own_hbm, own_ref), (blk_hbm, blk_ref), (cnt_hbm, cnt_ref), (force_hbm, force_ref), (vel_hbm, v)))]
     get_kern = [pltpu.make_async_copy(kern_hbm.at[pl.ds(g * span, span)], kv.at[pl.ds(g * span, span)],
                                       kern_sem.at[g]) for g in range(groups)]
     for copy in gets + get_kern:
         copy.start()
-
-    barrier = pltpu.get_barrier_semaphore()
-    for k in range(1, width):
-        pl.semaphore_signal(barrier, inc=1, device_id={"gy": lax.rem(me + k, width)}, device_id_type=MESH)
-    z_lo, z_hi = gz > 0, gz < depth - 1
-    y_lo, y_hi = me > 0, me < width - 1
-
-    @pl.when(z_lo)
-    def _():
-        pl.semaphore_signal(barrier, inc=1, device_id={"gz": gz - 1}, device_id_type=MESH)
-
-    @pl.when(z_hi)
-    def _():
-        pl.semaphore_signal(barrier, inc=1, device_id={"gz": gz + 1}, device_id_type=MESH)
 
     for copy in gets[:3]:
         copy.wait()
@@ -85,29 +85,18 @@
     tail = jnp.where(iota((total, 128), 1) < 64, id_lo, id_hi)
     id_out[...] = tail.reshape(width, room, 128).astype(bf16)
 
+    gets[3].wait()
+    line8 = iota((group, pts), 0)
+    for g in range(groups):
+        for c in range(comps):
+            rows_f = force_ref[c, g * group:(g + 1) * group, :].astype(f32)
+            for i in range(group):
+                left_ref[g, c * group:(c + 1) * group, i * pts:(i + 1) * pts] = jnp.where(
+                    line8 == i, rows_f, 0.0).astype(bf16)
     gets[4].wait()
     for c in range(comps):
         zs[0, c] = v[c, 0].astype(bf16)
         zs[1, c] = v[c, planes - 1].astype(bf16)
-        for side, y in ((0, 0), (1, rows - 1)):
-            ys[side, c] = jnp.concatenate([v[c, z, y:y + 1, :] for z in range(planes)], axis=0).astype(bf16)
-
-    pl.semaphore_wait(barrier, width - 1 + z_lo.astype(jnp.int32) + z_hi.astype(jnp.int32))
-
-    order = sorted(range(1, width), key=lambda k: -min(k, width - k))
-
-    def out(src, dst, send_sem, recv_sem, back_by=False):
-        copies = {}
-        for k in order:
-            shift = width - k if back_by else k
-            copies[k] = pltpu.make_async_remote_copy(
-                src_ref=src.at[k], dst_ref=dst.at[k], send_sem=send_sem.at[k], recv_sem=recv_sem.at[k],
-                device_id={"gy": lax.rem(me + shift, width)}, device_id_type=MESH)
-            copies[k].start()
-        return copies
-
-    tell = out(id_out, id_in, id_send, id_recv)
-    id_in[0] = id_out[0]
 
     def halo(src, dst, sem, axis, target):
         return pltpu.make_async_remote_copy(
@@ -118,25 +107,59 @@
     z_up = halo(zs.at[1], zr.at[0], 0, "gz", gz + 1)
     y_down = halo(ys.at[0], yr.at[1], 3, "gy", me - 1)
     y_up = halo(ys.at[1], yr.at[0], 2, "gy", me + 1)
-    for there, copy in ((z_lo, z_down), (z_hi, z_up), (y_lo, y_down), (y_hi, y_up)):
-        pl.when(there)(copy.start)
-
-    gets[3].wait()
-    line8 = iota((group, pts), 0)
+
+    def enter():
+        pl.semaphore_wait(barrier, width - 1 + z_lo.astype(jnp.int32) + z_hi.astype(jnp.int32))
+        for there, copy in ((z_lo, z_down), (z_hi, z_up)):
+            pl.when(there)(copy.start)
+
+    pl.when(me >= width // 2)(enter)
+    for c in range(comps):
+        for side, y in ((0, 0), (1, rows - 1)):
+            ys[side, c] = jnp.concatenate([v[c, z, y:y + 1, :] for z in range(planes)], axis=0).astype(bf16)
     parts = []
-    for g in range(groups):
-        left = jnp.concatenate([jnp.concatenate([
-            jnp.where(line8 == i, force_ref[c, g * group + i:g * group + i + 1, :].astype(f32), 0.0)
-            for i in range(group)], axis=1) for c in range(comps)], axis=0).astype(bf16)
-        get_kern[g].wait()
-        parts.append(jnp.dot(left, kv[g * span:(g + 1) * span, :], preferred_element_type=f32))
+    for pair in range(0, groups, 2):
+        both = range(pair, min(pair + 2, groups))
+        for g in both:
+            get_kern[g].wait()
+        for g in both:
+            parts.append(jnp.dot(left_ref[g], kv[g * span:(g + 1) * span, :], preferred_element_type=f32))
     spread = jnp.concatenate([
         jnp.concatenate([part[c * group:(c + 1) * group] for part in parts], axis=0)
         for c in range(comps)], axis=1).astype(bf16)
     placed = jnp.dot(jnp.where(chosen, 1.0, 0.0).astype(bf16), spread, preferred_element_type=f32)
     send[...] = placed.reshape(width, room, body).astype(bf16)
 
+    pl.when(me < width // 2)(enter)
+
+    after = width - 1 - me
+    right = (after >= me).astype(jnp.int32)
+    big = right * after + (1 - right) * me
+    small = width - 1 - big
+    others = range(1, width)
+    far_first = []
+    for j in range(width - 1):
+        one = (j < big - small).astype(jnp.int32)
+        rest = (1 - one) * (j - big + small)
+        step = one * (big - j) + (1 - one) * (small - rest // 2)
+        far_first.append(me + (2 * right - 1) * (1 - 2 * (rest % 2)) * step)
+
+    def out(src, dst, send_sem, recv_sem, back_by=False):
+        def copy(k, target):
+            return pltpu.make_async_remote_copy(
+                src_ref=src.at[k], dst_ref=dst.at[k], send_sem=send_sem.at[k], recv_sem=recv_sem.at[k],
+                device_id={"gy": target}, device_id_type=MESH)
+
+        for target in far_first:
+            gap = me - target if back_by else target - me
+            copy(lax.rem(gap + width, width), target).start()
+        return {k: copy(k, lax.rem(me + k, width)) for k in others}
+
+    tell = out(id_out, id_in, id_send, id_recv)
     go = out(send, recv, go_send, go_recv)
+    for there, copy in ((y_lo, y_down), (y_hi, y_up)):
+        pl.when(there)(copy.start)
+    id_in[0] = id_out[0]
     recv[0] = send[0]
 
     lane = iota((rows, xcells), 1)
@@ -182,7 +205,7 @@
                     w = coef + sign * v[1, z, y:y + 1, :]
                     fresh[c, z, y:y + 1, :] += w * got[z:z + 1, :]
 
-    for k in order[::-1]:
+    for k in others:
         tell[k].wait()
     gid = id_in[...].astype(f32).reshape(total, 128)
     gid = 128.0 * gid[:, 64:65] + gid[:, 0:1]
@@ -191,7 +214,7 @@
     place_c = (iota((total, zy), 1) * nx).astype(f32)
     puts = [jnp.where(place_r + float(b) == ids_r, time_step, 0.0).astype(bf16) for b in range(nx)]
     takes = [jnp.where(place_c + float(b) == gid, 1.0, 0.0).astype(bf16) for b in range(nx)]
-    for k in order[::-1]:
+    for k in others:
         go[k].wait()
     got = recv[...].astype(f32).reshape(total, body).astype(bf16)
     for b in range(nx):
@@ -213,7 +236,7 @@
     for there, copy in ((z_lo, z_down), (z_hi, z_up), (y_lo, y_down), (y_hi, y_up)):
         pl.when(there)(copy.wait_send)
     pick = jnp.where(iota((slots, total), 1).astype(f32) == slot_c, 1.0, 0.0).astype(bf16)
-    for k in order[::-1]:
+    for k in others:
         home[k].wait()
     held = mine[...].astype(f32).reshape(total, body).astype(bf16)
     held_ref[...] = jnp.dot(pick, held, preferred_element_type=f32).astype(bf16)
@@ -268,6 +291,7 @@
             pltpu.VMEM((1, slots), jnp.int32),
             pltpu.VMEM((1, 1), jnp.int32),
             pltpu.VMEM((comps, planes * rows, xcells), bf16),
+            pltpu.VMEM((slots // 8, comps * 8, 8 * pts), bf16),
             pltpu.VMEM((width, room, 128), bf16),
             pltpu.VMEM((width, room, 128), bf16),
             pltpu.VMEM((width, room, body), bf16),

time: 19.4 us -> 18.1 us (0.933)
  Pallas kernels: 18 us -> 16.6 us
    pallas_call x1, Pallas kernels: 16.2 us -> 14.8 us  [local(): pl.pallas_call(functools.partial(step_kernel, width, depth, room), out_sh...]
where the time goes in v1:
time: 18.1 us; the launch traced here: 17.9 us
  Pallas kernels  16.6 us (92%)
  between operations  1.29 us (7%)
    pallas_call x1, Pallas kernels, local(): pl.pallas_call(functools.partial(step_kernel, width, depth, room), out_sh...  14.8 us
    pallas_call x1, Pallas kernels, local(): pl.pallas_call(sample_kernel, out_shape=(jax.ShapeDtypeStruct(velocity.sh...  1.79 us

profile of v1, /device:TPU:0, one launch (start us, length us, event | category | flops | bytes accessed | tf_op | source)
XLA Modules:
  0.0 17.9 jit_solution(10250104395614978633)
XLA Ops:
  1.3 14.8 %boundary_step.1 = (f32[3,8,16,768]{3,2,1,0:T(8,128)S(1)}, bf16[4096,256]{1,0:T(8,128)(2,1)S(1)}, bf16[32,768]{1,0:T(8,128)(2,1)S(1)}) custom-call(f32[3,8,16,768]{3,2,1,0:T(8,128)} %vel_hbm.1, bf16[3,32,128]{2,1,0:T(8,128)(2,1)} %bitcast.8, bf16[4096,256]{1,0:T(8,128)(2,1)} %bitcast.7, s32[1,32]{1,0:T(1,128)} %bitcast.9, s32[1,32]{1,0:T(1,128)} %bitcast.10, ...), custom_call_target="tpu_custom_call" | custom-call | tf_op jit(solution)/shard_map/boundary_step/pallas_call | solution.py:278
  16.1 1.8 %sample_points.1 = (f32[3,8,16,768]{3,2,1,0:T(8,128)}, f32[3,32,128]{2,1,0:T(8,128)}) custom-call(f32[3,8,16,768]{3,2,1,0:T(8,128)S(1)} %get-tuple-element.7.fresh, bf16[4096,256]{1,0:T(8,128)(2,1)S(1)} %get-tuple-element.8.kv, bf16[32,768]{1,0:T(8,128)(2,1)S(1)} %get-tuple-element.9.held_ref), custom_call_target="tpu_custom_call" | custom-call | tf_op jit(solution)/shard_map/sample_points/pallas_call | solution.py:312

commit v2 on v1

--- a/solution.py
+++ b/solution.py
@@ -20,10 +20,10 @@
 
 
 def step_kernel(width, depth, room, vel_hbm, force_hbm, kern_hbm, own_hbm, blk_hbm, cnt_hbm,
-                fresh, kv, held_ref,
-                v, force_ref, own_ref, blk_ref, cnt_ref, cells16, left_ref, id_out, id_in, send, recv, back, mine,
+                fresh, kvt, held_ref,
+                v, kv, force_ref, own_ref, blk_ref, cnt_ref, cells16, left_ref, id_out, id_in, send, recv, back, mine,
                 zs, zr, ys, yr,
-                in_sem, kern_sem, id_send, id_recv, go_send, go_recv, re_send, re_recv, h_send, h_recv):
+                in_sem, kern_sem, id_sems, go_sems, re_sems, h_send, h_recv):
     me = lax.axis_index("gy")
     gz = lax.axis_index("gz")
     comps, planes, rows, xcells = v.shape
@@ -53,11 +53,17 @@
     def _():
         pl.semaphore_signal(barrier, inc=1, device_id={"gz": gz + 1}, device_id_type=MESH)
 
+    inner = pl.ds(1, planes - 2)
     gets = [pltpu.make_async_copy(src, dst, in_sem.at[i]) for i, (src, dst) in enumerate((
-        (own_hbm, own_ref), (blk_hbm, blk_ref), (cnt_hbm, cnt_ref), (force_hbm, force_ref), (vel_hbm, v)))]
-    get_kern = [pltpu.make_async_copy(kern_hbm.at[pl.ds(g * span, span)], kv.at[pl.ds(g * span, span)],
-                                      kern_sem.at[g]) for g in range(groups)]
-    for copy in gets + get_kern:
+        (own_hbm, own_ref), (blk_hbm, blk_ref), (cnt_hbm, cnt_ref), (force_hbm, force_ref),
+        (vel_hbm.at[:, 0], v.at[:, 0]), (vel_hbm.at[:, planes - 1], v.at[:, planes - 1]),
+        (vel_hbm.at[:, inner], v.at[:, inner])))]
+    halves = 2 if groups % 2 == 0 else 1
+    part_rows = groups // halves * span
+    get_kern = [pltpu.make_async_copy(kern_hbm.at[pl.ds(h * part_rows, part_rows)],
+                                      kv.at[pl.ds(h * part_rows, part_rows)], kern_sem.at[h])
+                for h in range(halves)]
+    for copy in gets[:6] + get_kern + gets[6:]:
         copy.start()
 
     for copy in gets[:3]:
@@ -94,6 +100,7 @@
                 left_ref[g, c * group:(c + 1) * group, i * pts:(i + 1) * pts] = jnp.where(
                     line8 == i, rows_f, 0.0).astype(bf16)
     gets[4].wait()
+    gets[5].wait()
     for c in range(comps):
         zs[0, c] = v[c, 0].astype(bf16)
         zs[1, c] = v[c, planes - 1].astype(bf16)
@@ -114,15 +121,10 @@
             pl.when(there)(copy.start)
 
     pl.when(me >= width // 2)(enter)
-    for c in range(comps):
-        for side, y in ((0, 0), (1, rows - 1)):
-            ys[side, c] = jnp.concatenate([v[c, z, y:y + 1, :] for z in range(planes)], axis=0).astype(bf16)
     parts = []
-    for pair in range(0, groups, 2):
-        both = range(pair, min(pair + 2, groups))
-        for g in both:
-            get_kern[g].wait()
-        for g in both:
+    for h in range(halves):
+        get_kern[h].wait()
+        for g in range(h * groups // halves, (h + 1) * groups // halves):
             parts.append(jnp.dot(left_ref[g], kv[g * span:(g + 1) * span, :], preferred_element_type=f32))
     spread = jnp.concatenate([
         jnp.concatenate([part[c * group:(c + 1) * group] for part in parts], axis=0)
@@ -130,13 +132,16 @@
     placed = jnp.dot(jnp.where(chosen, 1.0, 0.0).astype(bf16), spread, preferred_element_type=f32)
     send[...] = placed.reshape(width, room, body).astype(bf16)
 
+    gets[6].wait()
+    for c in range(comps):
+        for side, y in ((0, 0), (1, rows - 1)):
+            ys[side, c] = jnp.concatenate([v[c, z, y:y + 1, :] for z in range(planes)], axis=0).astype(bf16)
     pl.when(me < width // 2)(enter)
 
     after = width - 1 - me
     right = (after >= me).astype(jnp.int32)
     big = right * after + (1 - right) * me
     small = width - 1 - big
-    others = range(1, width)
     far_first = []
     for j in range(width - 1):
         one = (j < big - small).astype(jnp.int32)
@@ -144,19 +149,20 @@
         step = one * (big - j) + (1 - one) * (small - rest // 2)
         far_first.append(me + (2 * right - 1) * (1 - 2 * (rest % 2)) * step)
 
-    def out(src, dst, send_sem, recv_sem, back_by=False):
-        def copy(k, target):
-            return pltpu.make_async_remote_copy(
-                src_ref=src.at[k], dst_ref=dst.at[k], send_sem=send_sem.at[k], recv_sem=recv_sem.at[k],
-                device_id={"gy": target}, device_id_type=MESH)
-
+    def out(src, dst, sems, back_by=False):
         for target in far_first:
             gap = me - target if back_by else target - me
-            copy(lax.rem(gap + width, width), target).start()
-        return {k: copy(k, lax.rem(me + k, width)) for k in others}
-
-    tell = out(id_out, id_in, id_send, id_recv)
-    go = out(send, recv, go_send, go_recv)
+            k = lax.rem(gap + width, width)
+            pltpu.make_async_remote_copy(
+                src_ref=src.at[k], dst_ref=dst.at[k], send_sem=sems.at[0], recv_sem=sems.at[1],
+                device_id={"gy": target}, device_id_type=MESH).start()
+        rest = pl.ds(1, width - 1)
+        return pltpu.make_async_remote_copy(
+            src_ref=src.at[rest], dst_ref=dst.at[rest], send_sem=sems.at[0], recv_sem=sems.at[1],
+            device_id={"gy": far_first[0]}, device_id_type=MESH)
+
+    tell = out(id_out, id_in, id_sems)
+    go = out(send, recv, go_sems)
     for there, copy in ((y_lo, y_down), (y_hi, y_up)):
         pl.when(there)(copy.start)
     id_in[0] = id_out[0]
@@ -205,8 +211,7 @@
                     w = coef + sign * v[1, z, y:y + 1, :]
                     fresh[c, z, y:y + 1, :] += w * got[z:z + 1, :]
 
-    for k in others:
-        tell[k].wait()
+    tell.wait()
     gid = id_in[...].astype(f32).reshape(total, 128)
     gid = 128.0 * gid[:, 64:65] + gid[:, 0:1]
     ids_r = jnp.sum(jnp.where(iota((total, total), 0) == iota((total, total), 1), gid, 0.0), axis=0, keepdims=True)
@@ -214,8 +219,7 @@
     place_c = (iota((total, zy), 1) * nx).astype(f32)
     puts = [jnp.where(place_r + float(b) == ids_r, time_step, 0.0).astype(bf16) for b in range(nx)]
     takes = [jnp.where(place_c + float(b) == gid, 1.0, 0.0).astype(bf16) for b in range(nx)]
-    for k in others:
-        go[k].wait()
+    go.wait()
     got = recv[...].astype(f32).reshape(total, body).astype(bf16)
     for b in range(nx):
         part = jnp.dot(puts[b], got, preferred_element_type=f32)
@@ -230,36 +234,39 @@
             part += jnp.dot(takes[b], cells16[c, :, b * cells:(b + 1) * cells], preferred_element_type=f32)
         back[:, :, c * cells:(c + 1) * cells] = part.reshape(width, room, cells).astype(bf16)
 
-    home = out(back, mine, re_send, re_recv, True)
+    home = out(back, mine, re_sems, True)
     mine[0] = back[0]
 
+    for t in range(slots * pts // cells):
+        kvt[:, t * cells:(t + 1) * cells] = kv[t * cells:(t + 1) * cells, :].T
     for there, copy in ((z_lo, z_down), (z_hi, z_up), (y_lo, y_down), (y_hi, y_up)):
         pl.when(there)(copy.wait_send)
     pick = jnp.where(iota((slots, total), 1).astype(f32) == slot_c, 1.0, 0.0).astype(bf16)
-    for k in others:
-        home[k].wait()
+    home.wait()
     held = mine[...].astype(f32).reshape(total, body).astype(bf16)
     held_ref[...] = jnp.dot(pick, held, preferred_element_type=f32).astype(bf16)
 
 
-def sample_kernel(fresh, kv, held_ref, fresh_hbm, out_ref, out_sem):
+def sample_kernel(fresh, kvt, held_ref, fresh_hbm, out_hbm, out_ref, out_sem):
     comps, slots, pts = out_ref.shape
-    cells = kv.shape[1]
+    cells = kvt.shape[0]
     group = 8
-    put_v = pltpu.make_async_copy(fresh, fresh_hbm, out_sem)
+    put_v = pltpu.make_async_copy(fresh, fresh_hbm, out_sem.at[0])
     put_v.start()
     line8 = iota((group, pts), 0)
     for g in range(slots // group):
         part = held_ref[g * group:(g + 1) * group, :].astype(f32)
         left = jnp.concatenate([part[:, c * cells:(c + 1) * cells] for c in range(comps)], axis=0).astype(bf16)
-        result = lax.dot_general(left, kv[g * group * pts:(g + 1) * group * pts, :],
-                                 (((1,), (1,)), ((), ())), preferred_element_type=f32)
+        result = jnp.dot(left, kvt[:, g * group * pts:(g + 1) * group * pts], preferred_element_type=f32)
         for c in range(comps):
             value = jnp.zeros((group, pts), f32)
             for i in range(group):
                 value = jnp.where(line8 == i, result[c * group:(c + 1) * group, i * pts:(i + 1) * pts], value)
             out_ref[c, g * group:(g + 1) * group, :] = value
+    put_p = pltpu.make_async_copy(out_ref, out_hbm, out_sem.at[1])
+    put_p.start()
     put_v.wait()
+    put_p.wait()
 
 
 def local(velocity, forces, kernels, owners, blocks, counts):
@@ -273,19 +280,20 @@
     vmem = pl.BlockSpec(memory_space=pltpu.VMEM)
     anyw = pl.BlockSpec(memory_space=pltpu.HBM)
     dma = pltpu.SemaphoreType.DMA
-    each = dma((width,))
+    pair = dma((2,))
     kept = 4 * velocity.size + 2 * kernels.size + 2 * slots * body
-    fresh, kv, held = pl.pallas_call(
+    fresh, kvt, held = pl.pallas_call(
         functools.partial(step_kernel, width, depth, room),
         out_shape=(
             pltpu.VMEM(velocity.shape, f32),
-            pltpu.VMEM((slots * pts, cells), bf16),
+            pltpu.VMEM((cells, slots * pts), bf16),
             pltpu.VMEM((slots, body), bf16),
         ),
         in_specs=[anyw] * 6,
         out_specs=(vmem, vmem, vmem),
         scratch_shapes=[
             pltpu.VMEM(velocity.shape, f32),
+            pltpu.VMEM((slots * pts, cells), bf16),
             pltpu.VMEM((comps, slots, pts), bf16),
             pltpu.VMEM((1, slots), jnp.int32),
             pltpu.VMEM((1, slots), jnp.int32),
@@ -302,7 +310,7 @@
             pltpu.VMEM((2, comps, rows, xcells), bf16),
             pltpu.VMEM((2, comps, planes, xcells), bf16),
             pltpu.VMEM((2, comps, planes, xcells), bf16),
-            dma((5,)), dma((slots // 8,)), each, each, each, each, each, each, dma((4,)), dma((4,)),
+            dma((7,)), dma((2,)), pair, pair, pair, dma((4,)), dma((4,)),
         ],
         compiler_params=pltpu.CompilerParams(
             collective_id=0, has_side_effects=True, vmem_limit_bytes=vmem_bytes - kept - 512 * 1024),
@@ -316,11 +324,11 @@
             jax.ShapeDtypeStruct((comps, slots, pts), f32),
         ),
         in_specs=[vmem, vmem, vmem],
-        out_specs=(anyw, vmem),
-        scratch_shapes=[dma],
+        out_specs=(anyw, anyw),
+        scratch_shapes=[pltpu.VMEM((comps, slots, pts), f32), dma((2,))],
         compiler_params=pltpu.CompilerParams(vmem_limit_bytes=24 * 2**20),
         name="sample_points",
-    )(fresh, kv, held)
+    )(fresh, kvt, held)
     return fresh, sampled.transpose(1, 0, 2)
 
 

time: 18.1 us -> 16.7 us (0.923)
  Pallas kernels: 16.6 us -> 15.2 us
    pallas_call x1, Pallas kernels: 14.8 us -> 14.1 us  [local(): pl.pallas_call(functools.partial(step_kernel, width, depth, room), out_sh...]
    pallas_call x1, Pallas kernels: 1.79 us -> 1.11 us  [local(): pl.pallas_call(sample_kernel, out_shape=(jax.ShapeDtypeStruct(velocity.sh...]
where the time goes in v2:
time: 16.7 us; the launch traced here: 16.5 us
  Pallas kernels  15.2 us (91%)
  between operations  1.29 us (8%)
    pallas_call x1, Pallas kernels, local(): pl.pallas_call(functools.partial(step_kernel, width, depth, room), out_sh...  14.1 us
    pallas_call x1, Pallas kernels, local(): pl.pallas_call(sample_kernel, out_shape=(jax.ShapeDtypeStruct(velocity.sh...  1.11 us

profile of v2, /device:TPU:0, one launch (start us, length us, event | category | flops | bytes accessed | tf_op | source)
XLA Modules:
  0.0 16.5 jit_solution(12238435532536044475)
XLA Ops:
  1.3 14.1 %boundary_step.1 = (f32[3,8,16,768]{3,2,1,0:T(8,128)S(1)}, bf16[256,4096]{1,0:T(8,128)(2,1)S(1)}, bf16[32,768]{1,0:T(8,128)(2,1)S(1)}) custom-call(f32[3,8,16,768]{3,2,1,0:T(8,128)} %vel_hbm.1, bf16[3,32,128]{2,1,0:T(8,128)(2,1)} %bitcast.8, bf16[4096,256]{1,0:T(8,128)(2,1)} %bitcast.7, s32[1,32]{1,0:T(1,128)} %bitcast.9, s32[1,32]{1,0:T(1,128)} %bitcast.10, ...), custom_call_target="tpu_custom_call" | custom-call | tf_op jit(solution)/shard_map/boundary_step/pallas_call | solution.py:285
  15.4 1.1 %sample_points.1 = (f32[3,8,16,768]{3,2,1,0:T(8,128)}, f32[3,32,128]{2,1,0:T(8,128)}) custom-call(f32[3,8,16,768]{3,2,1,0:T(8,128)S(1)} %get-tuple-element.7.fresh, bf16[256,4096]{1,0:T(8,128)(2,1)S(1)} %get-tuple-element.8.kvt, bf16[32,768]{1,0:T(8,128)(2,1)S(1)} %get-tuple-element.9.held_ref), custom_call_target="tpu_custom_call" | custom-call | tf_op jit(solution)/shard_map/sample_points/pallas_call | solution.py:320

commit v3 on v2

--- a/solution.py
+++ b/solution.py
@@ -21,7 +21,7 @@
 
 def step_kernel(width, depth, room, vel_hbm, force_hbm, kern_hbm, own_hbm, blk_hbm, cnt_hbm,
                 fresh, kvt, held_ref,
-                v, kv, force_ref, own_ref, blk_ref, cnt_ref, cells16, left_ref, id_out, id_in, send, recv, back, mine,
+                v, kv, force_ref, own_ref, blk_ref, cnt_ref, cells16, edge, pre, left_ref, id_out, id_in, send, recv, back, mine,
                 zs, zr, ys, yr,
                 in_sem, kern_sem, id_sems, go_sems, re_sems, h_send, h_recv):
     me = lax.axis_index("gy")
@@ -57,13 +57,14 @@
     gets = [pltpu.make_async_copy(src, dst, in_sem.at[i]) for i, (src, dst) in enumerate((
         (own_hbm, own_ref), (blk_hbm, blk_ref), (cnt_hbm, cnt_ref), (force_hbm, force_ref),
         (vel_hbm.at[:, 0], v.at[:, 0]), (vel_hbm.at[:, planes - 1], v.at[:, planes - 1]),
+        (vel_hbm.at[:, :, 0], edge.at[0]), (vel_hbm.at[:, :, rows - 1], edge.at[1]),
         (vel_hbm.at[:, inner], v.at[:, inner])))]
     halves = 2 if groups % 2 == 0 else 1
     part_rows = groups // halves * span
     get_kern = [pltpu.make_async_copy(kern_hbm.at[pl.ds(h * part_rows, part_rows)],
                                       kv.at[pl.ds(h * part_rows, part_rows)], kern_sem.at[h])
                 for h in range(halves)]
-    for copy in gets[:6] + get_kern + gets[6:]:
+    for copy in gets[:8] + get_kern + gets[8:]:
         copy.start()
 
     for copy in gets[:3]:
@@ -85,11 +86,10 @@
     slot_c = slot_of(own_c, rank_c, iota((slots, 1), 0))
     slot_r = slot_of(own_r[0:1, :], rank_r, iota((1, slots), 1))
     chosen = iota((total, slots), 0).astype(f32) == slot_r
-    ids = jnp.sum(jnp.where(chosen, blk_ref[...].astype(f32), 0.0), axis=1, keepdims=True)
-    id_hi = jnp.floor(ids * (1.0 / 128.0))
-    id_lo = ids - 128.0 * id_hi
-    tail = jnp.where(iota((total, 128), 1) < 64, id_lo, id_hi)
-    id_out[...] = tail.reshape(width, room, 128).astype(bf16)
+    ids = jnp.sum(jnp.where(chosen, blk_ref[...].astype(f32) + 1.0, 0.0), axis=1, keepdims=True) - 1.0
+    slot_lane = iota((room, 128), 1) == iota((room, 128), 0)
+    for k in range(width):
+        id_out[k] = jnp.sum(jnp.where(slot_lane, ids[k * room:(k + 1) * room], 0.0), axis=0, keepdims=True)
 
     gets[3].wait()
     line8 = iota((group, pts), 0)
@@ -115,12 +115,26 @@
     y_down = halo(ys.at[0], yr.at[1], 3, "gy", me - 1)
     y_up = halo(ys.at[1], yr.at[0], 2, "gy", me + 1)
 
+    early = me >= width // 2
+    late = jnp.logical_not(early)
+
     def enter():
         pl.semaphore_wait(barrier, width - 1 + z_lo.astype(jnp.int32) + z_hi.astype(jnp.int32))
+
+    def start_z(when):
         for there, copy in ((z_lo, z_down), (z_hi, z_up)):
-            pl.when(there)(copy.start)
-
-    pl.when(me >= width // 2)(enter)
+            pl.when(jnp.logical_and(when, there))(copy.start)
+
+    def start_y(when):
+        for there, copy in ((y_lo, y_down), (y_hi, y_up)):
+            pl.when(jnp.logical_and(when, there))(copy.start)
+
+    pl.when(early)(enter)
+    start_z(early)
+    gets[6].wait()
+    gets[7].wait()
+    ys[...] = edge[...].astype(bf16)
+    start_y(early)
     parts = []
     for h in range(halves):
         get_kern[h].wait()
@@ -132,11 +146,8 @@
     placed = jnp.dot(jnp.where(chosen, 1.0, 0.0).astype(bf16), spread, preferred_element_type=f32)
     send[...] = placed.reshape(width, room, body).astype(bf16)
 
-    gets[6].wait()
-    for c in range(comps):
-        for side, y in ((0, 0), (1, rows - 1)):
-            ys[side, c] = jnp.concatenate([v[c, z, y:y + 1, :] for z in range(planes)], axis=0).astype(bf16)
-    pl.when(me < width // 2)(enter)
+    pl.when(late)(enter)
+    start_z(late)
 
     after = width - 1 - me
     right = (after >= me).astype(jnp.int32)
@@ -149,25 +160,28 @@
         step = one * (big - j) + (1 - one) * (small - rest // 2)
         far_first.append(me + (2 * right - 1) * (1 - 2 * (rest % 2)) * step)
 
-    def out(src, dst, sems, back_by=False):
-        for target in far_first:
+    def out(src, dst, sems, targets, back_by=False):
+        for target in targets:
             gap = me - target if back_by else target - me
             k = lax.rem(gap + width, width)
             pltpu.make_async_remote_copy(
                 src_ref=src.at[k], dst_ref=dst.at[k], send_sem=sems.at[0], recv_sem=sems.at[1],
                 device_id={"gy": target}, device_id_type=MESH).start()
+
+    def sent(src, dst, sems):
         rest = pl.ds(1, width - 1)
         return pltpu.make_async_remote_copy(
             src_ref=src.at[rest], dst_ref=dst.at[rest], send_sem=sems.at[0], recv_sem=sems.at[1],
             device_id={"gy": far_first[0]}, device_id_type=MESH)
 
-    tell = out(id_out, id_in, id_sems)
-    go = out(send, recv, go_sems)
-    for there, copy in ((y_lo, y_down), (y_hi, y_up)):
-        pl.when(there)(copy.start)
+    out(id_out, id_in, id_sems, far_first)
+    out(send, recv, go_sems, far_first[:2])
+    start_y(late)
+    out(send, recv, go_sems, far_first[2:])
     id_in[0] = id_out[0]
     recv[0] = send[0]
 
+    gets[8].wait()
     lane = iota((rows, xcells), 1)
     line = iota((rows, xcells), 0)
     first_x, last_x = lane == 0, lane == xcells - 1
@@ -193,14 +207,6 @@
 
     lax.fori_loop(0, planes, plane, 0)
 
-    for there, copy, buf, z, sign in ((z_lo, z_up, 0, 0, half), (z_hi, z_down, 1, planes - 1, -half)):
-        @pl.when(there)
-        def _(copy=copy, buf=buf, z=z, sign=sign):
-            copy.wait_recv()
-            w = coef + sign * v[2, z]
-            for c in range(comps):
-                fresh[c, z] += w * zr[buf, c].astype(f32)
-
     for there, copy, buf, y, sign in ((y_lo, y_up, 0, 0, half), (y_hi, y_down, 1, rows - 1, -half)):
         @pl.when(there)
         def _(copy=copy, buf=buf, y=y, sign=sign):
@@ -211,38 +217,61 @@
                     w = coef + sign * v[1, z, y:y + 1, :]
                     fresh[c, z, y:y + 1, :] += w * got[z:z + 1, :]
 
-    tell.wait()
-    gid = id_in[...].astype(f32).reshape(total, 128)
-    gid = 128.0 * gid[:, 64:65] + gid[:, 0:1]
-    ids_r = jnp.sum(jnp.where(iota((total, total), 0) == iota((total, total), 1), gid, 0.0), axis=0, keepdims=True)
-    place_r = (iota((zy, total), 0) * nx).astype(f32)
-    place_c = (iota((total, zy), 1) * nx).astype(f32)
-    puts = [jnp.where(place_r + float(b) == ids_r, time_step, 0.0).astype(bf16) for b in range(nx)]
-    takes = [jnp.where(place_c + float(b) == gid, 1.0, 0.0).astype(bf16) for b in range(nx)]
-    go.wait()
+    sent(id_out, id_in, id_sems).wait()
+    theirs = jnp.concatenate([jnp.broadcast_to(id_in[k], (room, 128)) for k in range(width)], axis=0)
+    slot_lane = iota((total, 128), 1) == iota((total, 128), 0) % room
+    theirs = jnp.sum(jnp.where(slot_lane, theirs, 0.0), axis=1, keepdims=True)
+    place = (iota((total, zy), 1) * nx).astype(f32)
+    takes = [jnp.where(place + float(b) == theirs, 1.0, 0.0).astype(bf16) for b in range(nx)]
+    every = jnp.concatenate(takes, axis=1)
+    match = lax.dot_general(every, every, (((1,), (1,)), ((), ())), preferred_element_type=f32)
+    match = (match * time_step).astype(bf16)
+    for there, copy, buf, z, sign in ((z_lo, z_up, 0, 0, half), (z_hi, z_down, 1, planes - 1, -half)):
+        @pl.when(there)
+        def _(copy=copy, buf=buf, z=z, sign=sign):
+            copy.wait_recv()
+            w = coef + sign * v[2, z]
+            for c in range(comps):
+                fresh[c, z] += w * zr[buf, c].astype(f32)
+
+    def split(z, carry):
+        at = pl.ds(pl.multiple_of(z * rows, rows), rows)
+        low = pl.ds(pl.multiple_of(zy + z * rows, rows), rows)
+        for c in range(comps):
+            value = fresh[c, z]
+            high = value.astype(bf16)
+            cells16[c, at, :] = high
+            cells16[c, low, :] = (value - high.astype(f32)).astype(bf16)
+        return carry
+
+    lax.fori_loop(0, planes, split, 0)
+
+    twice = [jnp.concatenate([take, take], axis=1) for take in takes]
+    for c in range(comps):
+        part = jnp.dot(twice[0], cells16[c, :, :cells], preferred_element_type=f32)
+        for b in range(1, nx):
+            part += jnp.dot(twice[b], cells16[c, :, b * cells:(b + 1) * cells], preferred_element_type=f32)
+        pre[:, c * cells:(c + 1) * cells] = part
+    sent(send, recv, go_sems).wait()
     got = recv[...].astype(f32).reshape(total, body).astype(bf16)
+    force = jnp.dot(match, got, preferred_element_type=f32)
+    back[...] = (pre[...] + force).reshape(width, room, body).astype(bf16)
+
+    out(back, mine, re_sems, far_first, True)
+    mine[0] = back[0]
+
     for b in range(nx):
-        part = jnp.dot(puts[b], got, preferred_element_type=f32)
+        put = (takes[b].astype(f32) * time_step).T.astype(bf16)
+        part = jnp.dot(put, got, preferred_element_type=f32)
         for c in range(comps):
             where = (c, slice(None), slice(None), slice(b * cells, (b + 1) * cells))
-            value = fresh[where] + part[:, c * cells:(c + 1) * cells].reshape(planes, rows, cells)
-            fresh[where] = value
-            cells16[c, :, b * cells:(b + 1) * cells] = value.reshape(zy, cells).astype(bf16)
-    for c in range(comps):
-        part = jnp.zeros((total, cells), f32)
-        for b in range(nx):
-            part += jnp.dot(takes[b], cells16[c, :, b * cells:(b + 1) * cells], preferred_element_type=f32)
-        back[:, :, c * cells:(c + 1) * cells] = part.reshape(width, room, cells).astype(bf16)
-
-    home = out(back, mine, re_sems, True)
-    mine[0] = back[0]
-
+            fresh[where] += part[:, c * cells:(c + 1) * cells].reshape(planes, rows, cells)
     for t in range(slots * pts // cells):
         kvt[:, t * cells:(t + 1) * cells] = kv[t * cells:(t + 1) * cells, :].T
     for there, copy in ((z_lo, z_down), (z_hi, z_up), (y_lo, y_down), (y_hi, y_up)):
         pl.when(there)(copy.wait_send)
     pick = jnp.where(iota((slots, total), 1).astype(f32) == slot_c, 1.0, 0.0).astype(bf16)
-    home.wait()
+    sent(back, mine, re_sems).wait()
     held = mine[...].astype(f32).reshape(total, body).astype(bf16)
     held_ref[...] = jnp.dot(pick, held, preferred_element_type=f32).astype(bf16)
 
@@ -298,10 +327,12 @@
             pltpu.VMEM((1, slots), jnp.int32),
             pltpu.VMEM((1, slots), jnp.int32),
             pltpu.VMEM((1, 1), jnp.int32),
-            pltpu.VMEM((comps, planes * rows, xcells), bf16),
+            pltpu.VMEM((comps, 2 * planes * rows, xcells), bf16),
+            pltpu.VMEM((2, comps, planes, xcells), f32),
+            pltpu.VMEM((total, body), f32),
             pltpu.VMEM((slots // 8, comps * 8, 8 * pts), bf16),
-            pltpu.VMEM((width, room, 128), bf16),
-            pltpu.VMEM((width, room, 128), bf16),
+            pltpu.VMEM((width, 1, 128), f32),
+            pltpu.VMEM((width, 1, 128), f32),
             pltpu.VMEM((width, room, body), bf16),
             pltpu.VMEM((width, room, body), bf16),
             pltpu.VMEM((width, room, body), bf16),
@@ -310,7 +341,7 @@
             pltpu.VMEM((2, comps, rows, xcells), bf16),
             pltpu.VMEM((2, comps, planes, xcells), bf16),
             pltpu.VMEM((2, comps, planes, xcells), bf16),
-            dma((7,)), dma((2,)), pair, pair, pair, dma((4,)), dma((4,)),
+            dma((9,)), dma((2,)), pair, pair, pair, dma((4,)), dma((4,)),
         ],
         compiler_params=pltpu.CompilerParams(
             collective_id=0, has_side_effects=True, vmem_limit_bytes=vmem_bytes - kept - 512 * 1024),

time: 16.7 us -> 16.2 us (0.970)
  Pallas kernels: 15.2 us -> 14.7 us
    pallas_call x1, Pallas kernels: 14.1 us -> 13.6 us  [local(): pl.pallas_call(functools.partial(step_kernel, width, depth, room), out_sh...]
where the time goes in v3:
time: 16.2 us; the launch traced here: 16 us
  Pallas kernels  14.7 us (91%)
  between operations  1.29 us (8%)
    pallas_call x1, Pallas kernels, local(): pl.pallas_call(functools.partial(step_kernel, width, depth, room), out_sh...  13.6 us
    pallas_call x1, Pallas kernels, local(): pl.pallas_call(sample_kernel, out_shape=(jax.ShapeDtypeStruct(velocity.sh...  1.11 us

profile of v3, /device:TPU:0, one launch (start us, length us, event | category | flops | bytes accessed | tf_op | source)
XLA Modules:
  0.0 16.0 jit_solution(1604201925112810846)
XLA Ops:
  1.3 13.6 %boundary_step.1 = (f32[3,8,16,768]{3,2,1,0:T(8,128)S(1)}, bf16[256,4096]{1,0:T(8,128)(2,1)S(1)}, bf16[32,768]{1,0:T(8,128)(2,1)S(1)}) custom-call(f32[3,8,16,768]{3,2,1,0:T(8,128)} %vel_hbm.1, bf16[3,32,128]{2,1,0:T(8,128)(2,1)} %bitcast.8, bf16[4096,256]{1,0:T(8,128)(2,1)} %bitcast.7, s32[1,32]{1,0:T(1,128)} %bitcast.9, s32[1,32]{1,0:T(1,128)} %bitcast.10, ...), custom_call_target="tpu_custom_call" | custom-call | tf_op jit(solution)/shard_map/boundary_step/pallas_call | solution.py:314
  14.9 1.1 %sample_points.1 = (f32[3,8,16,768]{3,2,1,0:T(8,128)}, f32[3,32,128]{2,1,0:T(8,128)}) custom-call(f32[3,8,16,768]{3,2,1,0:T(8,128)S(1)} %get-tuple-element.7.fresh, bf16[256,4096]{1,0:T(8,128)(2,1)S(1)} %get-tuple-element.8.kvt, bf16[32,768]{1,0:T(8,128)(2,1)S(1)} %get-tuple-element.9.held_ref), custom_call_target="tpu_custom_call" | custom-call | tf_op jit(solution)/shard_map/sample_points/pallas_call | solution.py:351

commit v4 on v3

--- a/solution.py
+++ b/solution.py
@@ -21,7 +21,7 @@
 
 def step_kernel(width, depth, room, vel_hbm, force_hbm, kern_hbm, own_hbm, blk_hbm, cnt_hbm,
                 fresh, kvt, held_ref,
-                v, kv, force_ref, own_ref, blk_ref, cnt_ref, cells16, edge, pre, left_ref, id_out, id_in, send, recv, back, mine,
+                v, kv, force_ref, own_ref, blk_ref, cnt_ref, cells16, edge, hz, pre, left_ref, id_out, id_in, send, recv, back, mine,
                 zs, zr, ys, yr,
                 in_sem, kern_sem, id_sems, go_sems, re_sems, h_send, h_recv):
     me = lax.axis_index("gy")
@@ -217,23 +217,6 @@
                     w = coef + sign * v[1, z, y:y + 1, :]
                     fresh[c, z, y:y + 1, :] += w * got[z:z + 1, :]
 
-    sent(id_out, id_in, id_sems).wait()
-    theirs = jnp.concatenate([jnp.broadcast_to(id_in[k], (room, 128)) for k in range(width)], axis=0)
-    slot_lane = iota((total, 128), 1) == iota((total, 128), 0) % room
-    theirs = jnp.sum(jnp.where(slot_lane, theirs, 0.0), axis=1, keepdims=True)
-    place = (iota((total, zy), 1) * nx).astype(f32)
-    takes = [jnp.where(place + float(b) == theirs, 1.0, 0.0).astype(bf16) for b in range(nx)]
-    every = jnp.concatenate(takes, axis=1)
-    match = lax.dot_general(every, every, (((1,), (1,)), ((), ())), preferred_element_type=f32)
-    match = (match * time_step).astype(bf16)
-    for there, copy, buf, z, sign in ((z_lo, z_up, 0, 0, half), (z_hi, z_down, 1, planes - 1, -half)):
-        @pl.when(there)
-        def _(copy=copy, buf=buf, z=z, sign=sign):
-            copy.wait_recv()
-            w = coef + sign * v[2, z]
-            for c in range(comps):
-                fresh[c, z] += w * zr[buf, c].astype(f32)
-
     def split(z, carry):
         at = pl.ds(pl.multiple_of(z * rows, rows), rows)
         low = pl.ds(pl.multiple_of(zy + z * rows, rows), rows)
@@ -246,19 +229,63 @@
 
     lax.fori_loop(0, planes, split, 0)
 
+    sent(id_out, id_in, id_sems).wait()
+    theirs = jnp.concatenate([jnp.broadcast_to(id_in[k], (room, 128)) for k in range(width)], axis=0)
+    slot_lane = iota((total, 128), 1) == iota((total, 128), 0) % room
+    theirs = jnp.sum(jnp.where(slot_lane, theirs, 0.0), axis=1, keepdims=True)
+    place = (iota((total, zy), 1) * nx).astype(f32)
+    takes = [jnp.where(place + float(b) == theirs, 1.0, 0.0).astype(bf16) for b in range(nx)]
+    column = iota((total, nx * 4 * rows), 1)
+    column_row = column % (2 * rows)
+    column_row += jnp.where(column_row < rows, 0, zy - 2 * rows)
+    column_id = (column_row * nx + column // (4 * rows)).astype(f32)
+    ends = jnp.where(column_id == theirs, 1.0, 0.0).astype(bf16)
+    every = jnp.concatenate(takes, axis=1)
+    match = lax.dot_general(every, every, (((1,), (1,)), ((), ())), preferred_element_type=f32)
+    match = (match * time_step).astype(bf16)
     twice = [jnp.concatenate([take, take], axis=1) for take in takes]
     for c in range(comps):
         part = jnp.dot(twice[0], cells16[c, :, :cells], preferred_element_type=f32)
         for b in range(1, nx):
             part += jnp.dot(twice[b], cells16[c, :, b * cells:(b + 1) * cells], preferred_element_type=f32)
         pre[:, c * cells:(c + 1) * cells] = part
+    z_sides = ((z_lo, z_up, 0, 0, half), (z_hi, z_down, 1, planes - 1, -half))
+    for there, copy, buf, z, sign in z_sides:
+        @pl.when(there)
+        def _(copy=copy, buf=buf, z=z, sign=sign):
+            copy.wait_recv()
+            w = coef + sign * v[2, z]
+            for c in range(comps):
+                value = w * zr[buf, c].astype(f32)
+                high = value.astype(bf16)
+                low = (value - high.astype(f32)).astype(bf16)
+                for b in range(nx):
+                    for part, at in ((high, buf * rows), (low, (2 + buf) * rows)):
+                        at += b * 4 * rows
+                        hz[at:at + rows, c * cells:(c + 1) * cells] = part[:, b * cells:(b + 1) * cells]
+
+        @pl.when(jnp.logical_not(there))
+        def _(buf=buf):
+            for b in range(nx):
+                for at in (buf * rows, (2 + buf) * rows):
+                    at += b * 4 * rows
+                    hz[at:at + rows, :] = jnp.zeros((rows, body), bf16)
+
     sent(send, recv, go_sems).wait()
     got = recv[...].astype(f32).reshape(total, body).astype(bf16)
-    force = jnp.dot(match, got, preferred_element_type=f32)
-    back[...] = (pre[...] + force).reshape(width, room, body).astype(bf16)
+    late_part = jnp.dot(jnp.concatenate([match, ends], axis=1), jnp.concatenate([got, hz[...]], axis=0),
+                        preferred_element_type=f32)
+    back[...] = (pre[...] + late_part).reshape(width, room, body).astype(bf16)
 
     out(back, mine, re_sems, far_first, True)
     mine[0] = back[0]
+
+    for there, copy, buf, z, sign in z_sides:
+        @pl.when(there)
+        def _(buf=buf, z=z, sign=sign):
+            w = coef + sign * v[2, z]
+            for c in range(comps):
+                fresh[c, z] += w * zr[buf, c].astype(f32)
 
     for b in range(nx):
         put = (takes[b].astype(f32) * time_step).T.astype(bf16)
@@ -329,6 +356,7 @@
             pltpu.VMEM((1, 1), jnp.int32),
             pltpu.VMEM((comps, 2 * planes * rows, xcells), bf16),
             pltpu.VMEM((2, comps, planes, xcells), f32),
+            pltpu.VMEM((xcells // cells * 4 * rows, body), bf16),
             pltpu.VMEM((total, body), f32),
             pltpu.VMEM((slots // 8, comps * 8, 8 * pts), bf16),
             pltpu.VMEM((width, 1, 128), f32),

time: 16.2 us -> 15.9 us (0.981)
  Pallas kernels: 14.7 us -> 14.5 us
    pallas_call x1, Pallas kernels: 13.6 us -> 13.4 us  [local(): pl.pallas_call(functools.partial(step_kernel, width, depth, room), out_sh...]
where the time goes in v4:
time: 15.9 us; the launch traced here: 15.8 us
  Pallas kernels  14.5 us (91%)
  between operations  1.29 us (8%)
    pallas_call x1, Pallas kernels, local(): pl.pallas_call(functools.partial(step_kernel, width, depth, room), out_sh...  13.4 us
    pallas_call x1, Pallas kernels, local(): pl.pallas_call(sample_kernel, out_shape=(jax.ShapeDtypeStruct(velocity.sh...  1.11 us

profile of v4, /device:TPU:0, one launch (start us, length us, event | category | flops | bytes accessed | tf_op | source)
XLA Modules:
  0.0 15.8 jit_solution(16971660044610255092)
XLA Ops:
  1.3 13.4 %boundary_step.1 = (f32[3,8,16,768]{3,2,1,0:T(8,128)S(1)}, bf16[256,4096]{1,0:T(8,128)(2,1)S(1)}, bf16[32,768]{1,0:T(8,128)(2,1)S(1)}) custom-call(f32[3,8,16,768]{3,2,1,0:T(8,128)} %vel_hbm.1, bf16[3,32,128]{2,1,0:T(8,128)(2,1)} %bitcast.8, bf16[4096,256]{1,0:T(8,128)(2,1)} %bitcast.7, s32[1,32]{1,0:T(1,128)} %bitcast.9, s32[1,32]{1,0:T(1,128)} %bitcast.10, ...), custom_call_target="tpu_custom_call" | custom-call | tf_op jit(solution)/shard_map/boundary_step/pallas_call | solution.py:341
  14.6 1.1 %sample_points.1 = (f32[3,8,16,768]{3,2,1,0:T(8,128)}, f32[3,32,128]{2,1,0:T(8,128)}) custom-call(f32[3,8,16,768]{3,2,1,0:T(8,128)S(1)} %get-tuple-element.7.fresh, bf16[256,4096]{1,0:T(8,128)(2,1)S(1)} %get-tuple-element.8.kvt, bf16[32,768]{1,0:T(8,128)(2,1)S(1)} %get-tuple-element.9.held_ref), custom_call_target="tpu_custom_call" | custom-call | tf_op jit(solution)/shard_map/sample_points/pallas_call | solution.py:379

commit v5 on v4

--- a/solution.py
+++ b/solution.py
@@ -21,7 +21,7 @@
 
 def step_kernel(width, depth, room, vel_hbm, force_hbm, kern_hbm, own_hbm, blk_hbm, cnt_hbm,
                 fresh, kvt, held_ref,
-                v, kv, force_ref, own_ref, blk_ref, cnt_ref, cells16, edge, hz, pre, left_ref, id_out, id_in, send, recv, back, mine,
+                v, kv, force_ref, index, cnt_ref, cells16, edge, hz, pre, left_ref, id_out, id_in, send, recv, back, mine,
                 zs, zr, ys, yr,
                 in_sem, kern_sem, id_sems, go_sems, re_sems, h_send, h_recv):
     me = lax.axis_index("gy")
@@ -54,11 +54,15 @@
         pl.semaphore_signal(barrier, inc=1, device_id={"gz": gz + 1}, device_id_type=MESH)
 
     inner = pl.ds(1, planes - 2)
-    gets = [pltpu.make_async_copy(src, dst, in_sem.at[i]) for i, (src, dst) in enumerate((
-        (own_hbm, own_ref), (blk_hbm, blk_ref), (cnt_hbm, cnt_ref), (force_hbm, force_ref),
-        (vel_hbm.at[:, 0], v.at[:, 0]), (vel_hbm.at[:, planes - 1], v.at[:, planes - 1]),
-        (vel_hbm.at[:, :, 0], edge.at[0]), (vel_hbm.at[:, :, rows - 1], edge.at[1]),
-        (vel_hbm.at[:, inner], v.at[:, inner])))]
+    gets = [pltpu.make_async_copy(src, dst, in_sem.at[i]) for i, src, dst in (
+        (0, own_hbm, index.at[pl.ds(0, 1)]), (0, blk_hbm, index.at[pl.ds(1, 1)]), (1, cnt_hbm, cnt_ref),
+        (2, force_hbm, force_ref),
+        (3, vel_hbm.at[:, 0], v.at[:, 0]), (3, vel_hbm.at[:, planes - 1], v.at[:, planes - 1]),
+        (4, vel_hbm.at[:, :, 0], edge.at[0]), (4, vel_hbm.at[:, :, rows - 1], edge.at[1]),
+        (5, vel_hbm.at[:, inner], v.at[:, inner]))]
+    both_index = pltpu.make_async_copy(index, index, in_sem.at[0])
+    both_planes = pltpu.make_async_copy(v.at[:, pl.ds(0, 2)], v.at[:, pl.ds(0, 2)], in_sem.at[3])
+    both_edges = pltpu.make_async_copy(edge, edge, in_sem.at[4])
     halves = 2 if groups % 2 == 0 else 1
     part_rows = groups // halves * span
     get_kern = [pltpu.make_async_copy(kern_hbm.at[pl.ds(h * part_rows, part_rows)],
@@ -67,10 +71,10 @@
     for copy in gets[:8] + get_kern + gets[8:]:
         copy.start()
 
-    for copy in gets[:3]:
-        copy.wait()
+    both_index.wait()
+    gets[2].wait()
     rowi, coli = iota((slots, slots), 0), iota((slots, slots), 1)
-    own_r = jnp.broadcast_to(own_ref[...].astype(f32), (slots, slots))
+    own_r = jnp.broadcast_to(index[0:1, :].astype(f32), (slots, slots))
     own_c = jnp.sum(jnp.where(rowi == coli, own_r, 0.0), axis=1, keepdims=True)
     same = jnp.where(own_r == own_c, 1.0, 0.0)
     rank_c = jnp.sum(jnp.where(coli < rowi, same, 0.0), axis=1, keepdims=True)
@@ -86,7 +90,7 @@
     slot_c = slot_of(own_c, rank_c, iota((slots, 1), 0))
     slot_r = slot_of(own_r[0:1, :], rank_r, iota((1, slots), 1))
     chosen = iota((total, slots), 0).astype(f32) == slot_r
-    ids = jnp.sum(jnp.where(chosen, blk_ref[...].astype(f32) + 1.0, 0.0), axis=1, keepdims=True) - 1.0
+    ids = jnp.sum(jnp.where(chosen, index[1:2, :].astype(f32) + 1.0, 0.0), axis=1, keepdims=True) - 1.0
     slot_lane = iota((room, 128), 1) == iota((room, 128), 0)
     for k in range(width):
         id_out[k] = jnp.sum(jnp.where(slot_lane, ids[k * room:(k + 1) * room], 0.0), axis=0, keepdims=True)
@@ -99,8 +103,7 @@
             for i in range(group):
                 left_ref[g, c * group:(c + 1) * group, i * pts:(i + 1) * pts] = jnp.where(
                     line8 == i, rows_f, 0.0).astype(bf16)
-    gets[4].wait()
-    gets[5].wait()
+    both_planes.wait()
     for c in range(comps):
         zs[0, c] = v[c, 0].astype(bf16)
         zs[1, c] = v[c, planes - 1].astype(bf16)
@@ -131,8 +134,7 @@
 
     pl.when(early)(enter)
     start_z(early)
-    gets[6].wait()
-    gets[7].wait()
+    both_edges.wait()
     ys[...] = edge[...].astype(bf16)
     start_y(early)
     parts = []
@@ -351,8 +353,7 @@
             pltpu.VMEM(velocity.shape, f32),
             pltpu.VMEM((slots * pts, cells), bf16),
             pltpu.VMEM((comps, slots, pts), bf16),
-            pltpu.VMEM((1, slots), jnp.int32),
-            pltpu.VMEM((1, slots), jnp.int32),
+            pltpu.VMEM((2, slots), jnp.int32),
             pltpu.VMEM((1, 1), jnp.int32),
             pltpu.VMEM((comps, 2 * planes * rows, xcells), bf16),
             pltpu.VMEM((2, comps, planes, xcells), f32),
@@ -369,7 +370,7 @@
             pltpu.VMEM((2, comps, rows, xcells), bf16),
             pltpu.VMEM((2, comps, planes, xcells), bf16),
             pltpu.VMEM((2, comps, planes, xcells), bf16),
-            dma((9,)), dma((2,)), pair, pair, pair, dma((4,)), dma((4,)),
+            dma((6,)), dma((2,)), pair, pair, pair, dma((4,)), dma((4,)),
         ],
         compiler_params=pltpu.CompilerParams(
             collective_id=0, has_side_effects=True, vmem_limit_bytes=vmem_bytes - kept - 512 * 1024),

time: 15.9 us -> 15.9 us (level)
  no operation moved by 1% of the time
where the time goes in v5:
time: 15.9 us; the launch traced here: 15.7 us
  Pallas kernels  14.4 us (91%)
  between operations  1.29 us (8%)
    pallas_call x1, Pallas kernels, local(): pl.pallas_call(functools.partial(step_kernel, width, depth, room), out_sh...  13.3 us
    pallas_call x1, Pallas kernels, local(): pl.pallas_call(sample_kernel, out_shape=(jax.ShapeDtypeStruct(velocity.sh...  1.11 us

profile of v5, /device:TPU:0, one launch (start us, length us, event | category | flops | bytes accessed | tf_op | source)
XLA Modules:
  0.0 15.7 jit_solution(15687662914945980407)
XLA Ops:
  1.3 13.3 %boundary_step.1 = (f32[3,8,16,768]{3,2,1,0:T(8,128)S(1)}, bf16[256,4096]{1,0:T(8,128)(2,1)S(1)}, bf16[32,768]{1,0:T(8,128)(2,1)S(1)}) custom-call(f32[3,8,16,768]{3,2,1,0:T(8,128)} %vel_hbm.1, bf16[3,32,128]{2,1,0:T(8,128)(2,1)} %bitcast.8, bf16[4096,256]{1,0:T(8,128)(2,1)} %bitcast.7, s32[1,32]{1,0:T(1,128)} %bitcast.9, s32[1,32]{1,0:T(1,128)} %bitcast.10, ...), custom_call_target="tpu_custom_call" | custom-call | tf_op jit(solution)/shard_map/boundary_step/pallas_call | solution.py:343
  14.6 1.1 %sample_points.1 = (f32[3,8,16,768]{3,2,1,0:T(8,128)}, f32[3,32,128]{2,1,0:T(8,128)}) custom-call(f32[3,8,16,768]{3,2,1,0:T(8,128)S(1)} %get-tuple-element.7.fresh, bf16[256,4096]{1,0:T(8,128)(2,1)S(1)} %get-tuple-element.8.kvt, bf16[32,768]{1,0:T(8,128)(2,1)S(1)} %get-tuple-element.9.held_ref), custom_call_target="tpu_custom_call" | custom-call | tf_op jit(solution)/shard_map/sample_points/pallas_call | solution.py:380
